TPU v7x, 32 devices: a whole 2x2x4 slice. The times are simulated.
32 devices in a mesh: row: 8 (over z, y), col: 4 (over x, core).
Axes of the slice: x: 2, y: 2, z: 4, core: 2. Of those that a mesh axis runs over, the one named last changes fastest.
Arguments:
- lower_panel: float32 [1, 4, 512, 4096], P(None, None, 'col', 'row'), may hold values from -4 to 4, as said below
- right_side: float32 [1, 4096, 4096], P(None, 'row', 'col'), may hold values from -6 to 6
Outputs:
- solution: float32 [4, 512, 4096], P(None, None, 'col')
- updated_rhs: float32 [1, 4096, 4096], P(None, 'row', 'col')
Inputs may be any that keep to these rules, and one draw needn't show every extreme that they name: `lower_panel`: L is lower triangular: entries of tiles L[g, s] with g < s and above the diagonal of L[s, s] are zero; the diagonal entries of L lie between 2 and 4.
All inputs are finite; a program needn't handle non-finite values.
Results may differ from a plain program's by a relative error of at most 0.00017.
Values sent between devices are 32-bit elements; how exact they have to be, the bound alone decides.
A program may use at most 128 MiB of HBM per device.

v0:
```python
import jax
import jax.numpy as jnp
from jax import lax
from jax.sharding import PartitionSpec as P


def from_root(x, axis, root):
    mine = lax.axis_index(axis) == root
    return lax.psum(jnp.where(mine, x, jnp.zeros_like(x)), axis)


def per_device(lower_panel, right_side):
    rounds = lower_panel.shape[0]
    sections = lower_panel.shape[1]
    block = lower_panel.shape[3]
    my_row = lax.axis_index("row")
    row_count = lax.axis_size("row")
    tile_number = jnp.arange(rounds, dtype=jnp.int32) * row_count + my_row
    current = right_side
    collected = []
    for section in range(sections):
        is_owner = my_row == section
        column = lax.dynamic_index_in_dim(lower_panel, section, 1, keepdims=False)
        diag_tile = lax.all_gather(column[0], "col", axis=0, tiled=True).T
        safe_tile = jnp.where(is_owner, diag_tile, jnp.eye(block, dtype=jnp.float32))
        local_solve = lax.linalg.triangular_solve(safe_tile, current[0], left_side=True, lower=True)
        solved = from_root(local_solve, "row", section)
        rows_here = solved
        update = jnp.einsum(
            "rcq,cx->rqx",
            lax.all_gather(column, "col", axis=1, tiled=True),
            rows_here,
            precision=lax.Precision.HIGHEST,
        )
        keep_rows = (tile_number > section)[:, None, None]
        current, solved = (current - jnp.where(keep_rows, update, jnp.float32(0.0)), solved)
        collected.append(solved)
    solutions = jnp.stack(collected)
    return (solutions, current)


def solution(mesh):
    placed = (P(None, None, "col", "row"), P(None, "row", "col"))
    return jax.shard_map(
        per_device,
        mesh=mesh,
        in_specs=placed,
        out_specs=(P(None, None, "col"), P(None, "row", "col")),
        check_vma=False,
    )
```

profile of v0, /device:TPU:0, one launch (start us, length us, event | category | flops | bytes accessed | tf_op | source)
XLA Modules:
  0.0 589.0 jit_solution(5360135936811088487)
XLA Ops:
  7.2 2.0 fusion.100
  9.2 0.8 copy.10
  10.1 0.8 copy.11
  11.1 18.7 %all-gather.13.cloned.1.call-done = f32[1,1,512,512]{2,3,1,0:T(8,128)} async-done(((f32[1,1,128,512]{2,3,1,0:T(8,128)}), f32[1,1,512,512]{2,3,1,0:T(8,128)}) %all-gather.13.cloned.1.call-update) | async-done | bytes 1048592 | tf_op jit(solution)/shard_map/all_gather | solution.py:24
  29.8 1.4 fusion.36
  31.1 0.7 broadcast.74.clone
  31.9 10.0 %while.8 = (s32[]{:T(128)}, f32[512,512]{1,0:T(8,128)S(1)}, s32[4,2]{0,1:T(2,128)S(1)}, f32[4,128,128]{2,1,0:T(8,128)}, s32[]{:T(128)}) while((s32[]{:T(128)}, f32[512,512]{1,0:T(8,128)S(1)}, s32[4,2]{0,1:T(2,128)S(1)}, f32[4,128,128]{2,1,0:T(8,128)}, s32[]{:T(128)}) %tuple.71), condition=%wide.while_cond, body=%wide.while_body.sunk | while | flops 2 | bytes 132205 | solution.py:26
  32.5 1.9 bitcast_dynamic-update-slice_fusion.8
  34.9 1.9 bitcast_dynamic-update-slice_fusion.8
  37.4 1.9 bitcast_dynamic-update-slice_fusion.8
  39.9 1.9 bitcast_dynamic-update-slice_fusion.8
  41.8 40.7 %custom-call.6 = f32[4,128,128]{1,2,0:T(8,128)} custom-call(f32[4,128,128]{2,1,0:T(8,128)} %get-tuple-element.29), custom_call_target="InvertDiagBlocksLowerTriangular" | custom-call | tf_op jit(solution)/shard_map/triangular_solve/custom-call.1 | solution.py:26
  82.6 1.5 fusion.62
  85.3 0.7 convolution_subtract_fusion.3
  86.7 1.1 fusion.33
  88.5 1.6 maximum_select_fusion
  90.1 0.9 copy-done.11
  91.0 0.8 copy.12
  91.9 1.8 copy.6
  93.7 1.4 fusion.37
  95.2 7.4 %while.9 = (s32[]{:T(128)}, f32[512,512]{1,0:T(8,128)S(1)}, s32[4,2]{0,1:T(2,128)S(1)}, f32[4,128,128]{2,1,0:T(8,128)S(1)}, s32[]{:T(128)}) while((s32[]{:T(128)}, f32[512,512]{1,0:T(8,128)S(1)}, s32[4,2]{0,1:T(2,128)S(1)}, f32[4,128,128]{2,1,0:T(8,128)S(1)}, s32[]{:T(128)}) %tuple.99), condition=%wide.while_cond.clone, body=%wide.while_body.clone.sunk | while | flops 2 | bytes 131189 | solution.py:26
  95.8 1.2 bitcast_dynamic-update-slice_fusion.9
  97.6 1.2 bitcast_dynamic-update-slice_fusion.9
  99.5 1.2 bitcast_dynamic-update-slice_fusion.9
  101.3 1.2 bitcast_dynamic-update-slice_fusion.9
  102.6 40.4 %custom-call.7 = f32[4,128,128]{1,2,0:T(8,128)} custom-call(f32[4,128,128]{2,1,0:T(8,128)S(1)} %get-tuple-element.30), custom_call_target="InvertDiagBlocksLowerTriangular" | custom-call | tf_op jit(solution)/shard_map/triangular_solve/custom-call.1 | solution.py:26
  143.0 49.6 %all-reduce.5.cloned.1.call-done = f32[512,1024]{1,0:T(8,128)} async-done(((f32[512,1024]{1,0:T(8,128)}), f32[512,1024]{1,0:T(8,128)}) %all-reduce.5.cloned.1.call-update) | async-done | bytes 2097168 | tf_op jit(solution)/shard_map/psum | solution.py:9
  192.6 8.9 %bitcast_subtract_fusion.3 = f32[1,512,1024]{1,2,0:T(8,128)S(1)} fusion(f32[1,512,1024]{1,2,0:T(8,128)} %copy.6, f32[512,1024]{1,0:T(8,128)} %all-reduce.5.cloned.1.call-done, f32[1,1,512,512]{2,3,1,0:T(8,128)S(1)} %copy-done.9, pred[]{:T(512)S(6)} %gt.16), kind=kOutput, calls=%fused_computation.20 | convolution fusion | flops 3222274048 | bytes 7340033 | tf_op jit(solution)/shard_map/rcq,cx->rqx/dot_general | solution.py:29
  202.2 1.8 convolution_subtract_fusion.6
  204.7 2.8 convolution_subtract_fusion.2
  208.1 3.9 fusion.30
  212.7 1.6 maximum_select_fusion.1
  214.3 0.9 copy.13
  215.3 2.3 fusion.38
  217.7 12.0 %while.10 = (s32[]{:T(128)}, f32[512,512]{1,0:T(8,128)}, s32[4,2]{0,1:T(2,128)S(1)}, f32[4,128,128]{2,1,0:T(8,128)S(1)}, s32[]{:T(128)}) while((s32[]{:T(128)}, f32[512,512]{1,0:T(8,128)}, s32[4,2]{0,1:T(2,128)S(1)}, f32[4,128,128]{2,1,0:T(8,128)S(1)}, s32[]{:T(128)}) %tuple.100), condition=%wide.while_cond.clone.1, body=%wide.while_body.clone.1.sunk | while | flops 2 | bytes 131189 | solution.py:26
  218.4 2.3 bitcast_dynamic-update-slice_fusion.10
  221.4 2.3 bitcast_dynamic-update-slice_fusion.10
  224.4 2.3 bitcast_dynamic-update-slice_fusion.10
  227.4 2.2 bitcast_dynamic-update-slice_fusion.10
  229.7 0.7 copy-done.15
  230.4 40.1 %custom-call.8 = f32[4,128,128]{1,2,0:T(8,128)S(1)} custom-call(f32[4,128,128]{2,1,0:T(8,128)} %copy-done.15), custom_call_target="InvertDiagBlocksLowerTriangular" | custom-call | tf_op jit(solution)/shard_map/triangular_solve/custom-call.1 | solution.py:26
  270.5 46.1 %all-reduce.7.cloned.1.call-done = f32[512,1024]{1,0:T(8,128)} async-done(((f32[512,1024]{1,0:T(8,128)}), f32[512,1024]{1,0:T(8,128)}) %all-reduce.7.cloned.1.call-update) | async-done | bytes 2097168 | tf_op jit(solution)/shard_map/psum | solution.py:9
  316.6 8.3 %bitcast_subtract_fusion.2 = f32[1,512,1024]{1,2,0:T(8,128)S(1)} fusion(f32[1,512,1024]{1,2,0:T(8,128)S(1)} %bitcast_subtract_fusion.3, f32[512,1024]{1,0:T(8,128)} %all-reduce.7.cloned.1.call-done, f32[1,1,512,512]{2,3,1,0:T(8,128)S(1)} %copy-done.6, pred[]{:T(512)S(6)} %gt.17), kind=kOutput, calls=%fused_computation.19 | convolution fusion | flops 3222274048 | bytes 7340033 | tf_op jit(solution)/shard_map/rcq,cx->rqx/dot_general | solution.py:29
  325.6 1.9 convolution_subtract_fusion.5
  328.2 2.8 convolution_subtract_fusion.1
  331.6 4.1 fusion.27
  336.4 1.6 maximum_select_fusion.2
  338.1 2.6 fusion.39
  340.7 11.2 %while.11 = (s32[]{:T(128)}, f32[512,512]{1,0:T(8,128)}, s32[4,2]{0,1:T(2,128)S(1)}, f32[4,128,128]{2,1,0:T(8,128)S(1)}, s32[]{:T(128)}) while((s32[]{:T(128)}, f32[512,512]{1,0:T(8,128)}, s32[4,2]{0,1:T(2,128)S(1)}, f32[4,128,128]{2,1,0:T(8,128)S(1)}, s32[]{:T(128)}) %tuple.101), condition=%wide.while_cond.clone.2, body=%wide.while_body.clone.2.sunk | while | flops 2 | bytes 131189 | solution.py:26
  341.3 2.2 bitcast_dynamic-update-slice_fusion.11
  344.1 2.2 bitcast_dynamic-update-slice_fusion.11
  346.9 2.2 bitcast_dynamic-update-slice_fusion.11
  349.8 2.1 bitcast_dynamic-update-slice_fusion.11
  352.6 40.1 %custom-call.9 = f32[4,128,128]{1,2,0:T(8,128)S(1)} custom-call(f32[4,128,128]{2,1,0:T(8,128)} %copy-done.14), custom_call_target="InvertDiagBlocksLowerTriangular" | custom-call | tf_op jit(solution)/shard_map/triangular_solve/custom-call.1 | solution.py:26
  392.7 48.1 %all-reduce.9.cloned.1.call-done = f32[512,1024]{1,0:T(8,128)} async-done(((f32[512,1024]{1,0:T(8,128)}), f32[512,1024]{1,0:T(8,128)}) %all-reduce.9.cloned.1.call-update) | async-done | bytes 2097168 | tf_op jit(solution)/shard_map/psum | solution.py:9
  440.8 8.3 %bitcast_subtract_fusion.1 = f32[1,512,1024]{1,2,0:T(8,128)S(1)} fusion(f32[1,512,1024]{1,2,0:T(8,128)S(1)} %copy-done.1, f32[512,1024]{1,0:T(8,128)} %all-reduce.9.cloned.1.call-done, f32[1,1,512,512]{2,3,1,0:T(8,128)S(1)} %copy-done.7, pred[]{:T(512)S(6)} %gt.18), kind=kOutput, calls=%fused_computation.18 | convolution fusion | flops 3222274048 | bytes 7340033 | tf_op jit(solution)/shard_map/rcq,cx->rqx/dot_general | solution.py:29
  449.8 1.9 convolution_subtract_fusion.4
  452.4 2.8 convolution_subtract_fusion
  455.8 3.9 fusion.24
  460.3 1.6 maximum_select_fusion.3
  461.9 101.7 %all-reduce.11.cloned.1.call-done = f32[512,1024]{1,0:T(8,128)} async-done(((f32[512,1024]{1,0:T(8,128)}), f32[512,1024]{1,0:T(8,128)}) %all-reduce.11.cloned.1.call-update) | async-done | bytes 2097168 | tf_op jit(solution)/shard_map/psum | solution.py:9
  563.6 9.6 %bitcast_subtract_fusion = f32[1,512,1024]{1,2,0:T(8,128)} fusion(f32[1,512,1024]{1,2,0:T(8,128)S(1)} %copy-done.3, f32[512,1024]{1,0:T(8,128)} %all-reduce.11.cloned.1.call-done, f32[1,1,512,512]{2,3,1,0:T(8,128)S(1)} %copy-done.8, pred[]{:T(512)S(6)} %gt.19), kind=kOutput, calls=%fused_computation.17 | convolution fusion | flops 3222274048 | bytes 7340033 | tf_op jit(solution)/shard_map/rcq,cx->rqx/dot_general | solution.py:29
  573.2 3.0 copy.9
  576.3 5.8 pad_maximum_fusion
  (102 shorter events, 21.4 us)
Async XLA Ops:
  7.2 22.6 %all-gather.13.cloned.1.call-start = ((), (), s32[]{:S(2)}) async-start(), calls=%async_computation.4 | async-start | bytes 1310720 | tf_op jit(solution)/shard_map/all_gather | solution.py:24
  10.0 72.5 %copy-start.4 = (f32[1,512,1024]{2,1,0:T(8,128)S(1)}, f32[1,512,1024]{2,1,0:T(8,128)}, u32[]{:S(2)}) copy-start(f32[1,512,1024]{2,1,0:T(8,128)} %param.5) | copy-start | bytes 6291460
  10.1 83.6 %all-gather.15.cloned.1.call-start = ((), (), s32[]{:S(2)}) async-start(), calls=%async_computation.5 | async-start | bytes 1310720 | tf_op jit(solution)/shard_map/all_gather | solution.py:24
  11.0 181.6 %all-reduce.5.cloned.1.call-start = ((), (), s32[]{:S(2)}) async-start(), calls=%async_computation | async-start | bytes 4194304 | tf_op jit(solution)/shard_map/psum | solution.py:9
  82.6 2.1 copy-start.13
  90.0 0.9 copy-start.11
  90.0 125.3 %all-gather.17.cloned.1.call-start = ((), (), s32[]{:S(2)}) async-start(), calls=%async_computation.6 | async-start | bytes 1310720 | tf_op jit(solution)/shard_map/all_gather | solution.py:24
  91.8 224.8 %all-reduce.7.cloned.1.call-start = ((), (), s32[]{:S(2)}) async-start(), calls=%async_computation.1 | async-start | bytes 4194304 | tf_op jit(solution)/shard_map/psum | solution.py:9
  93.7 98.9 %copy-start.9 = (f32[1,1,512,512]{2,3,1,0:T(8,128)S(1)}, f32[1,1,512,512]{2,3,1,0:T(8,128)}, u32[]{:S(2)}) copy-start(f32[1,1,512,512]{2,3,1,0:T(8,128)} %all-gather.13.cloned.1.call-done) | copy-start | bytes 3145732
  102.6 40.4 %copy-start.10 = (f32[512,512]{1,0:T(8,128)}, f32[512,512]{1,0:T(8,128)S(1)}, u32[]{:S(2)}) copy-start(f32[512,512]{1,0:T(8,128)S(1)} %get-tuple-element.280) | copy-start | bytes 3145732
  192.6 8.9 %copy-start.12 = (f32[4,128,128]{1,2,0:T(8,128)S(1)}, f32[4,128,128]{1,2,0:T(8,128)}, u32[]{:S(2)}) copy-start(f32[4,128,128]{1,2,0:T(8,128)} %custom-call.7) | copy-start | bytes 786436
  214.3 102.4 %copy-start.6 = (f32[1,1,512,512]{2,3,1,0:T(8,128)S(1)}, f32[1,1,512,512]{2,3,1,0:T(8,128)}, u32[]{:S(2)}) copy-start(f32[1,1,512,512]{2,3,1,0:T(8,128)} %all-gather.15.cloned.1.call-done) | copy-start | bytes 3145732
  214.3 123.8 %all-gather.19.cloned.1.call-start = ((), (), s32[]{:S(2)}) async-start(), calls=%async_computation.7 | async-start | bytes 1310720 | tf_op jit(solution)/shard_map/all_gather | solution.py:24
  215.2 225.6 %all-reduce.9.cloned.1.call-start = ((), (), s32[]{:S(2)}) async-start(), calls=%async_computation.2 | async-start | bytes 4194304 | tf_op jit(solution)/shard_map/psum | solution.py:9
  229.7 0.7 copy-start.15
  324.9 6.7 %copy-start = (f32[1,512,1024]{1,2,0:T(8,128)}, f32[1,512,1024]{1,2,0:T(8,128)S(1)}, u32[]{:S(2)}) copy-start(f32[1,512,1024]{1,2,0:T(8,128)S(1)} %bitcast_subtract_fusion.2) | copy-start | bytes 6291460
  337.9 102.9 %copy-start.7 = (f32[1,1,512,512]{2,3,1,0:T(8,128)S(1)}, f32[1,1,512,512]{2,3,1,0:T(8,128)}, u32[]{:S(2)}) copy-start(f32[1,1,512,512]{2,3,1,0:T(8,128)} %all-gather.17.cloned.1.call-done) | copy-start | bytes 3145732
  338.0 102.9 %copy-start.1 = (f32[1,512,1024]{1,2,0:T(8,128)S(1)}, f32[1,512,1024]{1,2,0:T(8,128)}, u32[]{:S(2)}) copy-start(f32[1,512,1024]{1,2,0:T(8,128)} %copy-done) | copy-start | bytes 6291460
  338.0 225.7 %all-reduce.11.cloned.1.call-start = ((), (), s32[]{:S(2)}) async-start(), calls=%async_computation.3 | async-start | bytes 4194304 | tf_op jit(solution)/shard_map/psum | solution.py:9
  351.9 0.7 copy-start.14
  449.1 6.6 %copy-start.2 = (f32[1,512,1024]{1,2,0:T(8,128)}, f32[1,512,1024]{1,2,0:T(8,128)S(1)}, u32[]{:S(2)}) copy-start(f32[1,512,1024]{1,2,0:T(8,128)S(1)} %bitcast_subtract_fusion.1) | copy-start | bytes 6291460
  460.3 103.3 %copy-start.8 = (f32[1,1,512,512]{2,3,1,0:T(8,128)S(1)}, f32[1,1,512,512]{2,3,1,0:T(8,128)}, u32[]{:S(2)}) copy-start(f32[1,1,512,512]{2,3,1,0:T(8,128)} %all-gather.19.cloned.1.call-done) | copy-start | bytes 3145732
  461.9 101.8 %copy-start.3 = (f32[1,512,1024]{1,2,0:T(8,128)S(1)}, f32[1,512,1024]{1,2,0:T(8,128)}, u32[]{:S(2)}) copy-start(f32[1,512,1024]{1,2,0:T(8,128)} %copy-done.2) | copy-start | bytes 6291460
  573.2 3.0 copy-start.5
Sparse Core Ops, SparseCore 0:
  10.2 19.5 all-gather.12
  31.3 16.9 all-gather.14
  90.2 102.4 all-reduce.4
  194.0 16.0 all-gather.16
  214.4 102.1 all-reduce.6
  318.0 16.0 all-gather.18
  338.3 102.4 all-reduce.8
  462.0 101.5 all-reduce.10
where the time goes:
time: 598 us; the launch traced here: 589 us
  waiting for transfers between devices  264 us (44%)
  other arithmetic  181 us (30%)
  matrix products  74.5 us (12%)
  local copies, waits for them, and re-layouts  53.6 us (9%)
  between operations  14.8 us (2%)
    psum x4, waiting for transfers between devices, from_root(): return lax.psum(jnp.where(mine, x, jnp.zeros_like(x)), axis)  246 us
    another operation x9, other arithmetic, per_device(): lax.linalg.triangular_solve(safe_tile, current[0], left_side=True, lower=...  169 us
    another operation x53, local copies, waits for them, and re-layouts, per_device(): lax.linalg.triangular_solve(safe_tile, current[0], left_side=True, lower=...  41.1 us
    another operation x28, matrix products, per_device(): lax.linalg.triangular_solve(safe_tile, current[0], left_side=True, lower=...  39.4 us
    dot_general x4, matrix products, per_device(): jnp.einsum('rcq,cx->rqx', lax.all_gather(column, 'col', axis=1, tiled=Tru...  35.1 us
    all_gather x4, waiting for transfers between devices, per_device(): diag_tile = lax.all_gather(column[0], 'col', axis=0, tiled=True).T  18.7 us
  transfers between devices with their start and end apart: 8, of which 5 were waited for; matrix products, arithmetic and copies ran while one was open for 45% of the time, Pallas kernels for 0%

commit v1 on v0

v1 whole, which is shorter than its diff:
```python
import functools

import jax
import jax.numpy as jnp
from jax import lax
from jax.experimental import pallas as pl
from jax.experimental.pallas import tpu as pltpu
from jax.sharding import PartitionSpec as P

MESH = pl.DeviceIdType.MESH
BASE = 32
WIDTH = 128
LAGS = (0, 1, 3, 5)


def dot(a, b):
    return jnp.dot(a, b, precision=lax.Precision.HIGHEST, preferred_element_type=jnp.float32)


def invert_unit(tile, n):
    row = lax.broadcasted_iota(jnp.int32, (n, n), 0)
    lane = lax.broadcasted_iota(jnp.int32, (n, n), 1)
    recip = 1.0 / jnp.sum(jnp.where(row == lane, tile, 0.0), axis=1, keepdims=True)
    inside = (row // BASE == lane // BASE) & (row > lane)
    fold = jnp.where(row % BASE == lane, 1.0, 0.0)
    coeff = dot(jnp.where(inside, tile * recip, 0.0), fold)
    blocks = n // BASE
    coeff = coeff.reshape(blocks, BASE, n)
    x = jnp.where(row == lane, recip, 0.0).reshape(blocks, BASE, n)
    for i in range(BASE - 1):
        x = x - coeff[:, :, i : i + 1] * x[:, i : i + 1, :]
    x = x.reshape(n, n)
    size = BASE
    while size < n:
        off = (row // size == lane // size + 1) & (row // (2 * size) == lane // (2 * size))
        x = x - dot(x, dot(jnp.where(off, tile, 0.0), x))
        size *= 2
    return x


def invert_into(low, inv):
    n = low.shape[0]
    inv[...] = jnp.zeros_like(inv)
    small = 128
    for k in range(n // small):
        at = pl.ds(k * small, small)
        inv[at, at] = invert_unit(low[at, at], small)
    size = small
    while size < n:
        for k in range(n // (2 * size)):
            top = pl.ds(2 * k * size, size)
            low_at = pl.ds((2 * k + 1) * size, size)
            inv[low_at, top] = -dot(inv[low_at, low_at], dot(low[low_at, top], inv[top, top]))
        size *= 2


def kernel(row_count, col_count, panel, rhs, sol, cur, tiles, low, inv,
           panel_send, panel_recv, hop_send, recv):
    sections, cw, n = panel.shape
    chunks = rhs.shape[1] // WIDTH
    row, col = lax.axis_index("row"), lax.axis_index("col")
    pos, plane = row // 2, row % 2
    line = row_count // 2
    partner = pos * 2 + (1 - plane)
    chips = col_count // 2
    chip, core = col // 2, col % 2
    twin = chip * 2 + (1 - core)
    up_row, down_row = jnp.minimum(row + 2, row_count - 1), jnp.maximum(row - 2, 0)
    has_up, has_down = pos < line - 1, pos > 0

    barrier = pltpu.get_barrier_semaphore()
    for step in range(1, chips):
        pl.semaphore_signal(barrier, inc=1, device_id=(row, lax.rem(chip + step, chips) * 2 + core), device_id_type=MESH)
    pl.semaphore_signal(barrier, inc=1, device_id=(row, twin), device_id_type=MESH)
    pl.semaphore_signal(barrier, inc=1, device_id=(partner, col), device_id_type=MESH)

    @pl.when(has_up)
    def _():
        pl.semaphore_signal(barrier, inc=1, device_id=(row + 2, col), device_id_type=MESH)

    @pl.when(has_down)
    def _():
        pl.semaphore_signal(barrier, inc=1, device_id=(row - 2, col), device_id_type=MESH)

    greeted = chips + 1 + jnp.where(has_up, 1, 0) + jnp.where(has_down, 1, 0)
    pl.semaphore_wait(barrier, greeted)

    def order(k):
        if k == 0:
            return jnp.where(row < sections, row, 0)
        return jnp.where((row < sections) & (k - 1 < row), k - 1, k)

    def piece(k, origin, source, target_col, slot):
        s = order(k)
        at = tiles.at[s, pl.ds(pl.multiple_of(origin * cw, cw), cw), :]
        return pltpu.make_async_remote_copy(
            src_ref=source if source is not None else at,
            dst_ref=at,
            send_sem=panel_send.at[k, slot],
            recv_sem=panel_recv.at[k, origin],
            device_id=(row, target_col),
            device_id_type=MESH,
        )

    sent = []
    for k in range(sections):
        own = panel.at[order(k)]
        for step in range(1, chips):
            c = piece(k, col, own, lax.rem(chip + step, chips) * 2 + core, step - 1)
            c.start()
            sent.append(c)
        c = piece(k, col, own, twin, chips - 1)
        c.start()
        sent.append(c)
    for s in range(sections):
        tiles[s, pl.ds(pl.multiple_of(col * cw, cw), cw), :] = panel[s]
    cur[...] = rhs[...]

    def collect(k):
        for step in range(1, chips):
            origin = lax.rem(chip + chips - step, chips) * 2 + core
            c = piece(k, origin, None, twin, chips - 1 + step)
            c.wait_recv()
            c.start()
            sent.append(c)
        for step in range(chips):
            origin = lax.rem(chip + step, chips) * 2 + (1 - core)
            piece(k, origin, None, twin, 0).wait_recv()

    collect(0)

    def columns(j):
        return pl.ds(pl.multiple_of(j * WIDTH, WIDTH), WIDTH)

    def hop(s, j, target, direction):
        at = sol.at[s, :, columns(j)]
        return pltpu.make_async_remote_copy(
            src_ref=at, dst_ref=at,
            send_sem=hop_send.at[direction, s, j],
            recv_sem=recv.at[s, j],
            device_id=(target, col), device_id_type=MESH,
        )

    def own_chunk(s, j):
        sol[s, :, columns(j)] = dot(inv[...], cur[:, columns(j)])
        hop(s, j, partner, 0).start()

        @pl.when(has_up)
        def _():
            hop(s, j, up_row, 1).start()

        @pl.when(has_down)
        def _():
            hop(s, j, down_row, 2).start()

    @pl.when(row < sections)
    def _():
        low[0] = tiles[order(0)].T
        invert_into(low.at[0], inv)

    @pl.when(row == 0)
    def _():
        @pl.loop(0, chunks)
        def _(j):
            own_chunk(0, j)

    for k in range(1, sections):
        collect(k)
    for s in range(sections):
        low[s] = tiles[s].T

    @pl.loop(0, chunks + LAGS[sections - 1])
    def _(t):
        for s in reversed(range(sections)):
            j = t - LAGS[s]

            @pl.when((j >= 0) & (j < chunks) & (row != s))
            def _(s=s, j=j):
                hop(s, j, partner, 0).wait_recv()

                @pl.when(plane == s % 2)
                def _():
                    @pl.when(has_up & (pos > s // 2))
                    def _():
                        hop(s, j, up_row, 1).start()

                    @pl.when(has_down & (pos < s // 2))
                    def _():
                        hop(s, j, down_row, 2).start()

                    hop(s, j, partner, 0).start()

                @pl.when(row > s)
                def _():
                    at = columns(j)
                    cur[:, at] = cur[:, at] - dot(low[s], sol[s, :, at])

                if s + 1 < sections:
                    @pl.when(row == s + 1)
                    def _():
                        own_chunk(s + 1, j)

    for c in sent:
        c.wait_send()
    for s in range(sections):
        @pl.when(plane == s % 2)
        def _(s=s):
            @pl.loop(0, chunks)
            def _(j):
                hop(s, j, partner, 0).wait_send()

                @pl.when(has_up & (pos >= s // 2))
                def _():
                    hop(s, j, up_row, 1).wait_send()

                @pl.when(has_down & (pos <= s // 2))
                def _():
                    hop(s, j, down_row, 2).wait_send()


def per_device(row_count, col_count, lower_panel, right_side):
    panel, rhs = lower_panel[0], right_side[0]
    sections, cw, n = panel.shape
    width = rhs.shape[1]
    chunks = width // WIDTH
    chips = col_count // 2
    vmem = pl.BlockSpec(memory_space=pltpu.VMEM)
    sol, cur = pl.pallas_call(
        functools.partial(kernel, row_count, col_count),
        out_shape=(
            jax.ShapeDtypeStruct((sections, n, width), jnp.float32),
            jax.ShapeDtypeStruct((n, width), jnp.float32),
        ),
        in_specs=[vmem, vmem],
        out_specs=(vmem, vmem),
        scratch_shapes=[
            pltpu.VMEM((sections, n, n), jnp.float32),
            pltpu.VMEM((sections, n, n), jnp.float32),
            pltpu.VMEM((n, n), jnp.float32),
            pltpu.SemaphoreType.DMA((sections, 2 * chips)),
            pltpu.SemaphoreType.DMA((sections, col_count)),
            pltpu.SemaphoreType.DMA((3, sections, chunks)),
            pltpu.SemaphoreType.DMA((sections, chunks)),
        ],
        compiler_params=pltpu.CompilerParams(
            collective_id=0, has_side_effects=True, vmem_limit_bytes=60 * 1024 * 1024
        ),
    )(panel, rhs)
    return sol, cur[None]


def solution(mesh):
    placed = (P(None, None, "col", "row"), P(None, "row", "col"))
    return jax.shard_map(
        functools.partial(per_device, mesh.shape["row"], mesh.shape["col"]),
        mesh=mesh,
        in_specs=placed,
        out_specs=(P(None, None, "col"), P(None, "row", "col")),
        check_vma=False,
    )
```

time: 598 us -> 316 us (0.53)
  the two profiles are of different devices: /device:TPU:0 before, /device:TPU:24 now
where the time goes in v1:
time: 316 us
  Pallas kernels  305 us (97%)
  local copies, waits for them, and re-layouts  9.91 us (3%)
    pallas_call x1, Pallas kernels, per_device(): pl.pallas_call(functools.partial(kernel, row_count, col_count), out_shape...  305 us
    unnamed x4, local copies, waits for them, and re-layouts  9.91 us

profile of v1, /device:TPU:24, one launch (start us, length us, event | category | flops | bytes accessed | tf_op | source)
XLA Modules:
  0.0 315.6 jit_solution(1956191957028742518)
XLA Ops:
  0.6 305.1 %shard_map.41 = (f32[4,512,1024]{2,1,0:T(8,128)}, f32[512,1024]{1,0:T(8,128)}) custom-call(f32[4,128,512]{2,1,0:T(8,128)} %bitcast.5, f32[512,1024]{1,0:T(8,128)} %bitcast.3), custom_call_target="tpu_custom_call" | custom-call | tf_op jit(solution)/shard_map/pallas_call | solution.py:228
  305.7 0.0 copy-start
  305.7 8.6 %copy.6 = f32[4,512,1024]{2,1,0:T(8,128)} copy(f32[4,512,1024]{2,1,0:T(8,128)} %get-tuple-element.8) | data formatting | bytes 16777216
  314.3 0.0 copy-done
  314.3 1.3 copy.7
Async XLA Ops:
  305.7 8.6 %copy-start = (f32[512,1024]{1,0:T(8,128)S(1)}, f32[512,1024]{1,0:T(8,128)}, u32[]{:S(2)}) copy-start(f32[512,1024]{1,0:T(8,128)} %get-tuple-element.5) | copy-start | bytes 6291460
